TPU v7x, 256 devices: a whole 4x4x8 slice. The times are simulated.
256 devices in a mesh: row: 16 (over y_hi, z), col: 16 (over x, y_lo, core).
Axes of the slice: x: 4, y: 4 (y_hi: 2, y_lo: 2; y = y_hi * 2 + y_lo), z: 8, core: 2. Of those that a mesh axis runs over, the one named last changes fastest.
Arguments:
- fields: float32 [1, 4, 256, 256, 256], P(None, None, 'row', 'col'), may hold values from -6 to 6
- cotangent: float32 [1, 4, 256, 256, 256], P(None, None, 'row', 'col'), may hold values from -6 to 6
- spec_weights: float32 [2, 4, 4, 16, 16, 16], replicated, may hold values from -96 to 96
- point_weights: float32 [4, 4], replicated, may hold values from -3 to 3
- bias: float32 [4], replicated, may hold values from -3 to 3
Outputs:
- grad_fields: float32 [1, 4, 256, 256, 256], P(None, None, 'row', 'col')
- grad_spectral: float32 [2, 4, 4, 16, 16, 16], replicated
All inputs are finite; a program needn't handle non-finite values.
Results may differ from a plain program's by a relative error of at most 0.00011.
Values sent between devices are 32-bit elements; how exact they have to be, the bound alone decides.
A program may use at most 64 MiB of HBM per device.

v0:
```python
import math

import jax
import jax.numpy as jnp
from jax import lax
from jax.sharding import PartitionSpec as P

C = 4
NX = 256
NY = 256
NZ = 256
MX = 16
MY = 16
MZ = 16


highest = lax.Precision.HIGHEST


def phase_tables(number, length, signed, start, count):
    wavenum = jnp.arange(number, dtype=jnp.int32)
    if signed:
        wavenum = jnp.where(wavenum < number // 2, wavenum, wavenum + length - number)
    points = start + jnp.arange(count, dtype=jnp.int32)
    angles = (
        2.0 * math.pi / length * (points[:, None] * wavenum[None, :] % length).astype(jnp.float32)
    )
    return (jnp.cos(angles), jnp.sin(angles))


def forward_table(number, length, start, count):
    cosine, sine = phase_tables(number, length, True, start, count)
    return jnp.stack([jnp.stack([cosine, -sine], 1), jnp.stack([sine, cosine], 1)], 0)


def inverse_table(number, length, start, count):
    cosine, sine = phase_tables(number, length, True, start, count)
    cosine = cosine.T
    sine = sine.T
    return jnp.stack([jnp.stack([cosine, sine], 1), jnp.stack([-sine, cosine], 1)], 0)


def first_table():
    cos_x, sin_x = phase_tables(MX, NX, False, 0, NX)
    return jnp.stack([cos_x, -sin_x], 1)


def last_table():
    cos_x, sin_x = phase_tables(MX, NX, False, 0, NX)
    wavenum = jnp.arange(MX, dtype=jnp.int32)
    weighting = jnp.where(wavenum == 0, 1.0, 2.0).astype(jnp.float32) / float(NX * NY * NZ)
    return jnp.stack([cos_x.T * weighting[:, None], -sin_x.T * weighting[:, None]], 0)


def to_modes(field):
    along_x = jnp.einsum("bcyzx,xtp->btpczy", field, first_table(), precision=highest)
    gathered = lax.all_to_all(along_x, "row", split_axis=2, concat_axis=5, tiled=True)
    along_y = jnp.einsum(
        "bspczy,sytq->btpcqz", gathered, forward_table(MY, NY, 0, NY), precision=highest
    )
    swapped = lax.all_to_all(along_y, "col", split_axis=4, concat_axis=5, tiled=True)
    return jnp.einsum(
        "bspcqz,sztr->btpcqr", swapped, forward_table(MZ, NZ, 0, NZ), precision=highest
    )


def from_modes(modes):
    along_z = jnp.einsum(
        "bspcqr,srtz->btpcqz", modes, inverse_table(MZ, NZ, 0, NZ), precision=highest
    )
    swapped = lax.all_to_all(along_z, "col", split_axis=5, concat_axis=4, tiled=True)
    along_y = jnp.einsum(
        "bspcqz,sqty->btpczy", swapped, inverse_table(MY, NY, 0, NY), precision=highest
    )
    gathered = lax.all_to_all(along_y, "row", split_axis=5, concat_axis=2, tiled=True)
    return jnp.einsum("btpczy,tpx->bcyzx", gathered, last_table(), precision=highest)


def per_device(fields, cotangent, spec_weights, point_weights, bias):
    row_pos = lax.axis_index("row")
    col_pos = lax.axis_index("col")
    zero_index = jnp.zeros((), jnp.int32)
    kx_local = MX // lax.axis_size("row")
    ky_local = MY // lax.axis_size("col")
    starts = (
        zero_index,
        zero_index,
        zero_index,
        row_pos * kx_local,
        col_pos * ky_local,
        zero_index,
    )
    owned_weights = lax.dynamic_slice(spec_weights, starts, (2, C, C, kx_local, ky_local, MZ))
    kx_start = row_pos * kx_local
    weight_real = owned_weights[0]
    weight_imag = owned_weights[1]
    spectrum_u = to_modes(fields)
    input_real = spectrum_u[:, 0]
    input_imag = spectrum_u[:, 1]
    mix_form = "bpiqr,iopqr->bpoqr"
    mixed_real = jnp.einsum(mix_form, input_real, weight_real, precision=highest) - jnp.einsum(
        mix_form, input_imag, weight_imag, precision=highest
    )
    mixed_imag = jnp.einsum(mix_form, input_real, weight_imag, precision=highest) + jnp.einsum(
        mix_form, input_imag, weight_real, precision=highest
    )
    spectral_term = from_modes(jnp.stack([mixed_real, mixed_imag], 1))
    local_term = jnp.einsum("bcyzx,co->boyzx", fields, point_weights, precision=highest)
    pre_activation = spectral_term + local_term + bias[None, :, None, None, None]
    gelu_slope = 0.5 * (1.0 + lax.erf(pre_activation / math.sqrt(2.0))) + pre_activation * jnp.exp(
        -0.5 * pre_activation * pre_activation
    ) / math.sqrt(2.0 * math.pi)
    upstream = cotangent * gelu_slope
    spectrum_h = to_modes(upstream)
    back_real = spectrum_h[:, 0]
    back_imag = spectrum_h[:, 1]
    grad_form = "bpiqr,bpoqr->iopqr"
    grad_real = jnp.einsum(grad_form, input_real, back_real, precision=highest) + jnp.einsum(
        grad_form, input_imag, back_imag, precision=highest
    )
    grad_imag = jnp.einsum(grad_form, input_real, back_imag, precision=highest) - jnp.einsum(
        grad_form, input_imag, back_real, precision=highest
    )
    wave_global = kx_start + jnp.arange(kx_local, dtype=jnp.int32)
    factor = jnp.where(wave_global == 0, 1.0, 2.0).astype(jnp.float32) / float(NX * NY * NZ)
    grad_block = jnp.stack([grad_real, grad_imag], 0) * factor[None, None, None, :, None, None]
    adj_form = "iopqr,bpoqr->bpiqr"
    adjoint_real = jnp.einsum(adj_form, weight_real, back_real, precision=highest) + jnp.einsum(
        adj_form, weight_imag, back_imag, precision=highest
    )
    adjoint_imag = jnp.einsum(adj_form, weight_real, back_imag, precision=highest) - jnp.einsum(
        adj_form, weight_imag, back_real, precision=highest
    )
    grad_fields = from_modes(jnp.stack([adjoint_real, adjoint_imag], 1))
    grad_fields = grad_fields + jnp.einsum(
        "boyzx,co->bcyzx", upstream, point_weights, precision=highest
    )
    full_grad = jnp.zeros((2, C, C, MX, MY, MZ), jnp.float32)
    full_grad = lax.dynamic_update_slice(full_grad, grad_block, starts)
    grad_spectral = lax.psum(full_grad, ("row", "col"))
    return (grad_fields, grad_spectral)


def solution(mesh):
    placed = (P(None, None, "row", "col", None), P(None, None, "row", "col", None), P(), P(), P())
    return jax.shard_map(
        per_device,
        mesh=mesh,
        in_specs=placed,
        out_specs=(P(None, None, "row", "col", None), P()),
        check_vma=False,
    )
```

profile of v0, /device:TPU:1, one launch (start us, length us, event | category | flops | bytes accessed | tf_op | source)
XLA Modules:
  0.0 426.7 jit_solution(5578637302729846114)
XLA Ops:
  7.3 1.1 copy-done
  8.4 4.4 %convolution_bitcast_fusion.3 = f32[1,2,16,4,16,16]{4,2,5,3,1,0:T(8,128)S(1)} fusion(f32[1,4,16,16,256]{4,3,2,1,0:T(8,128)S(1)} %copy-done, f32[256,1,16]{0,2,1:T(8,128)S(1)} %get-tuple-element.46, f32[256,1,16]{0,2,1:T(8,128)S(1)} %get-tuple-element.47), kind=kOutput, calls=%fused_computation.7 | convolution fusion | flops 100671488 | bytes 1212416 | tf_op jit(solution)/shard_map/bcyzx,xtp->btpczy/dot_general | solution.py:56
  13.2 1.0 reshape.708
  14.2 11.7 %all-to-all-start = ((f32[16,1,2048]{2,1,0:T(1,128)}), f32[16,1,2048]{2,1,0:T(1,128)S(1)}, u32[]{:S(2)}, u32[]{:S(2)}) async-start(f32[16,1,2048]{2,1,0:T(1,128)} %reshape.708), calls=%async_computation | async-start | bytes 262144 | tf_op jit(solution)/shard_map/all_to_all | solution.py:57
  26.3 8.6 %all-to-all-done = f32[16,1,2048]{2,1,0:T(1,128)S(1)} async-done(((f32[16,1,2048]{2,1,0:T(1,128)}), f32[16,1,2048]{2,1,0:T(1,128)S(1)}, u32[]{:S(2)}, u32[]{:S(2)}) %all-to-all-start) | async-done | bytes 131104 | tf_op jit(solution)/shard_map/all_to_all | solution.py:57
  35.4 0.9 reduce.16
  37.8 0.7 convolution_bitcast_fusion.7
  38.5 0.7 reshape.710
  39.2 6.5 %all-to-all-start.1 = ((f32[16,1,128]{2,1,0:T(1,128)}), f32[16,1,128]{2,1,0:T(1,128)S(1)}, u32[]{:S(2)}, u32[]{:S(2)}) async-start(f32[16,1,128]{2,1,0:T(1,128)} %reshape.710), calls=%async_computation.1 | async-start | bytes 16384 | tf_op jit(solution)/shard_map/all_to_all | solution.py:61
  45.7 0.9 constant_dynamic-slice_fusion.1
  46.6 4.6 %all-to-all-done.1 = f32[16,1,128]{2,1,0:T(1,128)S(1)} async-done(((f32[16,1,128]{2,1,0:T(1,128)}), f32[16,1,128]{2,1,0:T(1,128)S(1)}, u32[]{:S(2)}, u32[]{:S(2)}) %all-to-all-start.1) | async-done | bytes 8224 | tf_op jit(solution)/shard_map/all_to_all | solution.py:61
  51.1 0.6 reduce.17
  52.8 1.0 reshape.712
  53.8 3.9 all-to-all-start.2
  57.7 2.8 fusion.16
  60.5 2.7 all-to-all-done.2
  63.2 0.6 reduce.18
  65.4 1.5 reshape.714
  66.8 3.8 all-to-all-start.3
  70.7 8.7 %all-to-all-done.3 = f32[16,1,2048]{2,1,0:T(1,128)S(1)} async-done(((f32[16,1,2048]{2,1,0:T(1,128)}), f32[16,1,2048]{2,1,0:T(1,128)S(1)}, u32[]{:S(2)}, u32[]{:S(2)}) %all-to-all-start.3) | async-done | bytes 131104 | tf_op jit(solution)/shard_map/all_to_all | solution.py:75
  79.4 0.9 reduce.19
  80.3 0.7 reshape.715
  81.0 2.2 copy.86
  83.2 4.0 fusion.8
  87.2 4.2 convolution_bitcast_fusion.1
  92.2 12.3 %all_to_all.96 = f32[16,1,2048]{2,1,0:T(1,128)S(1)} all-to-all(f32[16,1,2048]{2,1,0:T(1,128)S(1)} %reshape.716), channel_id=1, replica_groups=mesh['row'=16,'col'=16] {'row'}, dimensions={0} | all-to-all | bytes 262144 | tf_op jit(solution)/shard_map/all_to_all | solution.py:57
  104.6 0.9 reduce.20
  105.9 1.1 bitcast_bitcast_fusion
  106.9 1.7 copy.188
  109.1 0.7 convolution_bitcast_fusion.6
  109.9 10.8 %all_to_all.97 = f32[16,1,128]{2,1,0:T(1,128)S(1)} all-to-all(f32[16,1,128]{2,1,0:T(1,128)S(1)} %reshape.718), channel_id=1, replica_groups=mesh['row'=16,'col'=16] {'col'}, dimensions={0} | all-to-all | bytes 16384 | tf_op jit(solution)/shard_map/all_to_all | solution.py:61
  120.7 0.6 reduce.21
  122.4 1.0 reshape.720
  123.3 3.9 all-to-all-start.6
  127.3 5.5 %all-to-all-done.6 = f32[16,1,128]{2,1,0:T(1,128)S(1)} async-done(((f32[16,1,128]{2,1,0:T(1,128)}), f32[16,1,128]{2,1,0:T(1,128)S(1)}, u32[]{:S(2)}, u32[]{:S(2)}) %all-to-all-start.6) | async-done | bytes 8224 | tf_op jit(solution)/shard_map/all_to_all | solution.py:71
  135.0 1.5 reshape.722
  136.4 3.5 all-to-all-start.7
  140.0 2.6 fusion.13
  142.6 2.5 broadcast_in_dim.14
  145.1 1.6 dynamic_update_slice.3
  146.8 2.2 all-to-all-done.7
  148.9 0.9 reduce.23
  149.9 1.7 reshape.723
  151.6 2.2 copy.103
  153.8 1.4 fusion
  155.2 1.6 copy.108
  156.8 258.4 %all-reduce.2.cloned.1.call-done = f32[2,4,4,16,16,16]{5,4,3,2,1,0:T(8,128)} async-done(((f32[2,4,4,16,16,16]{5,4,3,2,1,0:T(8,128)}), f32[2,4,4,16,16,16]{5,4,3,2,1,0:T(8,128)}) %all-reduce.2.cloned.1.call-update) | async-done | bytes 524304 | tf_op jit(solution)/shard_map/psum | solution.py:140
  415.2 4.7 %copy.228 = f32[2,4,4,16,16,16]{5,4,3,2,1,0:T(8,128)} copy(f32[2,4,4,16,16,16]{5,4,3,2,1,0:T(8,128)} %all-reduce.2.cloned.1.call-done) | data formatting | bytes 1048576
  (58 shorter events, 10.2 us)
Async XLA Ops:
  7.2 1.2 copy-start
  14.2 20.7 %all-to-all-start = ((f32[16,1,2048]{2,1,0:T(1,128)}), f32[16,1,2048]{2,1,0:T(1,128)S(1)}, u32[]{:S(2)}, u32[]{:S(2)}) async-start(f32[16,1,2048]{2,1,0:T(1,128)} %reshape.708), calls=%async_computation | async-start | bytes 262144 | tf_op jit(solution)/shard_map/all_to_all | solution.py:57
  35.4 22.3 %copy-start.1 = (f32[4,4]{1,0:T(4,128)S(1)}, f32[4,4]{1,0:T(4,128)}, u32[]{:S(2)}) copy-start(f32[4,4]{1,0:T(4,128)} %param.8) | copy-start | bytes 196
  39.2 12.0 %all-to-all-start.1 = ((f32[16,1,128]{2,1,0:T(1,128)}), f32[16,1,128]{2,1,0:T(1,128)S(1)}, u32[]{:S(2)}, u32[]{:S(2)}) async-start(f32[16,1,128]{2,1,0:T(1,128)} %reshape.710), calls=%async_computation.1 | async-start | bytes 16384 | tf_op jit(solution)/shard_map/all_to_all | solution.py:61
  53.8 9.4 %all-to-all-start.2 = ((f32[16,1,128]{2,1,0:T(1,128)}), f32[16,1,128]{2,1,0:T(1,128)S(1)}, u32[]{:S(2)}, u32[]{:S(2)}) async-start(f32[16,1,128]{2,1,0:T(1,128)} %reshape.712), calls=%async_computation.2 | async-start | bytes 16384 | tf_op jit(solution)/shard_map/all_to_all | solution.py:71
  57.7 25.5 %copy-start.2 = (f32[4]{0:T(128)S(1)}, f32[4]{0:T(128)}, u32[]{:S(2)}) copy-start(f32[4]{0:T(128)} %param.9) | copy-start | bytes 52
  66.8 12.5 %all-to-all-start.3 = ((f32[16,1,2048]{2,1,0:T(1,128)}), f32[16,1,2048]{2,1,0:T(1,128)S(1)}, u32[]{:S(2)}, u32[]{:S(2)}) async-start(f32[16,1,2048]{2,1,0:T(1,128)} %reshape.714), calls=%async_computation.3 | async-start | bytes 262144 | tf_op jit(solution)/shard_map/all_to_all | solution.py:75
  123.3 9.4 %all-to-all-start.6 = ((f32[16,1,128]{2,1,0:T(1,128)}), f32[16,1,128]{2,1,0:T(1,128)S(1)}, u32[]{:S(2)}, u32[]{:S(2)}) async-start(f32[16,1,128]{2,1,0:T(1,128)} %reshape.720), calls=%async_computation.6 | async-start | bytes 16384 | tf_op jit(solution)/shard_map/all_to_all | solution.py:71
  136.4 12.5 %all-to-all-start.7 = ((f32[16,1,2048]{2,1,0:T(1,128)}), f32[16,1,2048]{2,1,0:T(1,128)S(1)}, u32[]{:S(2)}, u32[]{:S(2)}) async-start(f32[16,1,2048]{2,1,0:T(1,128)} %reshape.722), calls=%async_computation.7 | async-start | bytes 262144 | tf_op jit(solution)/shard_map/all_to_all | solution.py:75
  140.0 275.2 %all-reduce.2.cloned.1.call-start = ((), (), s32[]{:S(2)}) async-start(), calls=%async_computation.8 | async-start | bytes 8388608 | tf_op jit(solution)/shard_map/psum | solution.py:140
Sparse Core Ops, SparseCore 0:
  146.9 268.2 all-reduce.1
where the time goes:
time: 428 us; the launch traced here: 427 us
  waiting for transfers between devices  291 us (68%)
  local copies, waits for them, and re-layouts  35.6 us (8%)
  starting transfers between devices  33.5 us (8%)
  blocking collectives  23.2 us (5%)
  matrix products  22.5 us (5%)
  between operations  14.5 us (3%)
  other arithmetic  6.94 us (2%)
    psum x1, waiting for transfers between devices, per_device(): grad_spectral = lax.psum(full_grad, ('row', 'col'))  258 us
    unnamed x26, local copies, waits for them, and re-layouts  18.6 us
    all_to_all x1, blocking collectives, to_modes(): lax.all_to_all(along_x, 'row', split_axis=2, concat_axis=5, tiled=True)  12.3 us
    all_to_all x1, starting transfers between devices, to_modes(): lax.all_to_all(along_x, 'row', split_axis=2, concat_axis=5, tiled=True)  11.7 us
    all_to_all x1, blocking collectives, to_modes(): lax.all_to_all(along_y, 'col', split_axis=4, concat_axis=5, tiled=True)  10.8 us
    all_to_all x2, waiting for transfers between devices, from_modes(): lax.all_to_all(along_y, 'row', split_axis=5, concat_axis=2, tiled=True)  10.8 us
    dot_general x2, matrix products, to_modes(): jnp.einsum('bcyzx,xtp->btpczy', field, first_table(), precision=highest)  8.67 us
    all_to_all x1, waiting for transfers between devices, to_modes(): lax.all_to_all(along_x, 'row', split_axis=2, concat_axis=5, tiled=True)  8.57 us
  transfers between devices with their start and end apart: 7, of which 7 were waited for; matrix products, arithmetic and copies ran while one was open for 4% of the time, Pallas kernels for 0%

commit v1 on v0

v1 whole, which is shorter than its diff:
```python
import functools
import math

import jax
import jax.numpy as jnp
import numpy as np
from jax import lax
from jax.experimental import pallas as pl
from jax.experimental.pallas import tpu as pltpu
from jax.sharding import PartitionSpec as P

C = 4
N = 256
MODES = 16
CELLS = 256
LINES = 16
PLANE = 32
DEPTH = 8
MESH = pl.DeviceIdType.MESH
f32 = jnp.float32
bf16 = jnp.bfloat16
NT = (((1,), (1,)), ((), ()))


def signed_table(outer):
    wave = np.where(np.arange(MODES) < MODES // 2, np.arange(MODES), np.arange(MODES) - MODES)
    points = np.arange(N)
    angle = 2.0 * np.pi / N * (points[:, None] * wave[None, :] % N)
    angle = np.repeat(angle, MODES, 1) if outer else np.tile(angle, (1, MODES))
    return np.concatenate([np.cos(angle), np.sin(angle)], 1).astype(np.float32)


def split_constant(table):
    high = table.astype(jnp.bfloat16)
    low = (table - high.astype(np.float64)).astype(jnp.bfloat16)
    return high, low


def x_angles():
    return 2.0 * np.pi / N * (np.arange(MODES)[:, None] * np.arange(N)[None, :] % N)


def analysis_constant():
    angle = x_angles()
    high, low = split_constant(np.concatenate([np.cos(angle), -np.sin(angle)], 0))
    return np.concatenate([high, low], 0)


def synthesis_constant():
    angle = x_angles()
    weight = np.where(np.arange(MODES) == 0, 1.0, 2.0)[:, None] / float(N) ** 3
    high, low = split_constant(np.concatenate([np.cos(angle) * weight, -np.sin(angle) * weight], 0))
    full = np.zeros((C, 384, N), high.dtype)
    for c in range(C):
        full[c, c * 32 : c * 32 + 32] = high
        full[c, 128 + c * 32 : 128 + c * 32 + 32] = high
        full[c, 256 + c * 32 : 256 + c * 32 + 32] = low
    return full


def halves(value):
    high = value.astype(bf16)
    low = (value - high.astype(f32)).astype(bf16)
    return high, low


def dot(a, b):
    return jnp.dot(a, b, preferred_element_type=f32)


def dot_nt(a, b):
    return lax.dot_general(a, b, NT, preferred_element_type=f32)


def analyse_x(tx, block):
    high, low = halves(block)
    both = dot_nt(tx[...], high)
    return both[:32] + both[32:] + dot_nt(tx[0:32, :], low)


def analyse_yz(lines, eh, el, tiles):
    high, low = halves(lines[...])
    both = dot(jnp.concatenate([high, low], 0), eh[...])
    part = both[:128] + both[128:] + dot(high, el[...])
    for c in range(C):
        re = part[c * 32 : c * 32 + 16]
        im = part[c * 32 + 16 : c * 32 + 32]
        pair = (re[:, :256] + im[:, 256:], im[:, :256] - re[:, 256:])
        for t in range(2):
            for half in range(2):
                for side in range(2):
                    tiles[t * 16 + (c * 2 + half) * 2 + side] = pair[t][
                        half * 8 : half * 8 + 8, side * 128 : side * 128 + 128
                    ]


def spectrum_of(tiles, t, c):
    rows = []
    for half in range(2):
        k = t * 16 + (c * 2 + half) * 2
        rows.append(jnp.concatenate([tiles[k], tiles[k + 1]], 1))
    return jnp.concatenate(rows, 0)


def synth_yz(modes, eh, el):
    rows = []
    for re, im in modes:
        rows.append(jnp.concatenate([re, -im], 1))
        rows.append(jnp.concatenate([im, re], 1))
    high, low = halves(jnp.concatenate(rows, 0))
    both = dot_nt(eh[...], jnp.concatenate([high, low], 0))
    lines = both[:, :128] + both[:, 128:] + dot_nt(el[...], high)
    high, low = halves(lines)
    return jnp.concatenate([high, low, high], 1)


def device_of(z, rank):
    return {"row": rank // 16 * DEPTH + z, "col": lax.rem(rank, 16)}


def comm_kernel(
    fields,
    cot,
    weights,
    ty,
    tz,
    tx_in,
    ts_in,
    point,
    bias,
    local_out,
    su_out,
    sh_out,
    wm_out,
    eh_out,
    el_out,
    fv,
    cv,
    lv,
    wv,
    tyv,
    tzv,
    tx,
    ts,
    lines,
    part_u,
    part_h,
    rs_u,
    rs_h,
    zs_u,
    zs_h,
    zr_u,
    zr_h,
    ag_u,
    ag_h,
    load_sem,
    send_sem,
    recv_sem,
):
    row = lax.axis_index("row")
    col = lax.axis_index("col")
    z = lax.rem(row, DEPTH)
    me = row // DEPTH * 16 + col

    loads = [
        pltpu.make_async_copy(ty.at[pl.ds(pl.multiple_of(row * LINES, 8), LINES)], tyv, load_sem.at[0]),
        pltpu.make_async_copy(tz.at[pl.ds(pl.multiple_of(col * LINES, 8), LINES)], tzv, load_sem.at[1]),
        pltpu.make_async_copy(tx_in, tx, load_sem.at[2]),
    ]
    for c in range(C):
        spot = pl.ds(c * CELLS, CELLS)
        loads.append(pltpu.make_async_copy(fields.at[spot], fv.at[spot], load_sem.at[3 + c]))
    loads.append(pltpu.make_async_copy(weights, wv, load_sem.at[7]))
    loads.append(pltpu.make_async_copy(ts_in, ts, load_sem.at[8]))
    loads.append(pltpu.make_async_copy(cot, cv, load_sem.at[9]))
    for load in loads:
        load.start()

    barrier = pltpu.get_barrier_semaphore()

    def greet_plane(step, carry):
        peer = lax.rem(me + step, PLANE)
        pl.semaphore_signal(barrier, inc=1, device_id=device_of(z, peer), device_id_type=MESH)
        return carry

    lax.fori_loop(1, PLANE, greet_plane, 0)

    def greet_depth(step, carry):
        peer = lax.rem(z + step, DEPTH)
        pl.semaphore_signal(barrier, inc=1, device_id=device_of(peer, me), device_id_type=MESH)
        return carry

    lax.fori_loop(1, DEPTH, greet_depth, 0)

    for k in range(3):
        loads[k].wait()
    cz = tzv[:, :256]
    sz = tzv[:, 256:]
    for y in range(LINES):
        cy = tyv[y : y + 1, :256]
        sy = tyv[y : y + 1, 256:]
        high, low = halves(jnp.concatenate([cy * cz - sy * sz, sy * cz + cy * sz], 1))
        eh_out[y * LINES : (y + 1) * LINES, :] = high
        el_out[y * LINES : (y + 1) * LINES, :] = low

    for c in range(C):
        loads[3 + c].wait()
        lines[c * 32 : c * 32 + 32, :] = analyse_x(tx, fv[c * CELLS : (c + 1) * CELLS, :])
    analyse_yz(lines, eh_out, el_out, part_u)

    pl.semaphore_wait(barrier, PLANE - 1 + DEPTH - 1)

    def copy_to(src, dst, sem, device):
        return pltpu.make_async_remote_copy(
            src_ref=src,
            dst_ref=dst,
            send_sem=send_sem.at[sem],
            recv_sem=recv_sem.at[sem],
            device_id=device,
            device_id_type=MESH,
        )

    def start_scatter(part, rs, sem):
        def send(step, carry):
            peer = lax.rem(me + step, PLANE)
            copy_to(part.at[peer], rs.at[me], sem, device_of(z, peer)).start()
            return carry

        lax.fori_loop(1, PLANE, send, 0)
        rs[me] = part[me]

    def finish_scatter(part, rs, sem):
        both = copy_to(
            part.at[pl.ds(0, PLANE - 1)], rs.at[pl.ds(0, PLANE - 1)], sem, device_of(z, me)
        )
        both.wait_recv()
        return both

    def exchange_depth(total, zs, zr, sem):
        zs[0] = total
        zr[z] = total

        def send(step, carry):
            peer = lax.rem(z + step, DEPTH)
            copy_to(zs.at[0], zr.at[z], sem, device_of(peer, me)).start()
            return carry

        lax.fori_loop(1, DEPTH, send, 0)
        both = copy_to(
            zr.at[pl.ds(0, DEPTH - 1)], zr.at[pl.ds(0, DEPTH - 1)], sem, device_of(z, me)
        )
        both.wait_recv()
        return both

    def gather_plane(total, zs, ag, sem):
        zs[1] = total
        ag[me] = total

        def send(step, carry):
            peer = lax.rem(me + step, PLANE)
            copy_to(zs.at[1], ag.at[me], sem, device_of(z, peer)).start()
            return carry

        lax.fori_loop(1, PLANE, send, 0)
        both = copy_to(
            ag.at[pl.ds(0, PLANE - 1)], ag.at[pl.ds(0, PLANE - 1)], sem, device_of(z, me)
        )
        both.wait_recv()
        return both

    def sum_tiles(ref, count):
        values = [ref[k] for k in range(count)]
        while len(values) > 1:
            values = [values[k] + values[k + 1] for k in range(0, len(values), 2)]
        return values[0]

    def finish_reduce(part, rs, zs, zr, ag, sem):
        done = [finish_scatter(part, rs, sem)]
        done.append(exchange_depth(sum_tiles(rs, PLANE), zs, zr, sem + 1))
        done.append(gather_plane(sum_tiles(zr, DEPTH), zs, ag, sem + 2))
        return done

    start_scatter(part_u, rs_u, 0)

    def local_terms(block, carry):
        at = block * 32
        inputs = [fv[pl.ds(pl.multiple_of(i * CELLS + at, 8), 32), :] for i in range(C)]
        for o in range(C):
            value = inputs[0] * point[0, o] + bias[o]
            for i in range(1, C):
                value = value + inputs[i] * point[i, o]
            lv[pl.ds(pl.multiple_of(o * CELLS + at, 8), 32), :] = value
        return carry

    lax.fori_loop(0, CELLS // 32, local_terms, 0)
    loads[7].wait()
    for q in range(MODES):
        wm_out[:, q * 16 : q * 16 + 16] = wv[pl.ds(q, 512, stride=MODES), :]
    loads[8].wait()
    loads[9].wait()

    done = finish_reduce(part_u, rs_u, zs_u, zr_u, ag_u, 0)

    def weight(t, i, o):
        at = ((t * C + i) * C + o) * MODES
        return wm_out[at : at + MODES, :]

    modes = []
    for o in range(C):
        re = im = 0.0
        for i in range(C):
            ur, ui = spectrum_of(ag_u, 0, i), spectrum_of(ag_u, 1, i)
            wr, wi = weight(0, i, o), weight(1, i, o)
            re = re + (ur * wr - ui * wi)
            im = im + (ur * wi + ui * wr)
        modes.append((re, im))
    synth = synth_yz(modes, eh_out, el_out)

    for c in range(C):
        base = c * CELLS
        lv[base : base + CELLS, :] += dot(synth, ts[c])

        def slope(block, carry):
            at = pl.ds(pl.multiple_of(base + block * 32, 8), 32)
            v = lv[at, :]
            cdf = 0.5 * (1.0 + lax.erf(v * (1.0 / math.sqrt(2.0))))
            density = jnp.exp(-0.5 * v * v) * (1.0 / math.sqrt(2.0 * math.pi))
            cv[at, :] = cv[at, :] * (cdf + v * density)
            return carry

        lax.fori_loop(0, CELLS // 32, slope, 0)
        lines[c * 32 : c * 32 + 32, :] = analyse_x(tx, cv[base : base + CELLS, :])
    analyse_yz(lines, eh_out, el_out, part_h)

    start_scatter(part_h, rs_h, 3)

    def back_terms(block, carry):
        at = block * 32
        outputs = [cv[pl.ds(pl.multiple_of(o * CELLS + at, 8), 32), :] for o in range(C)]
        for i in range(C):
            value = outputs[0] * point[i, 0]
            for o in range(1, C):
                value = value + outputs[o] * point[i, o]
            local_out[pl.ds(pl.multiple_of(i * CELLS + at, 8), 32), :] = value
        return carry

    lax.fori_loop(0, CELLS // 32, back_terms, 0)
    for k in range(PLANE):
        su_out[k] = ag_u[k]

    done += finish_reduce(part_h, rs_h, zs_h, zr_h, ag_h, 3)
    for k in range(PLANE):
        sh_out[k] = ag_h[k]
    for both in done:
        both.wait_send()


def final_kernel(local, su, sh, wm, eh, el, ts, grad_fields, grad_weights):
    def weight(t, i, o):
        at = ((t * C + i) * C + o) * MODES
        return wm[at : at + MODES, :]

    modes = []
    for i in range(C):
        re = im = 0.0
        for o in range(C):
            hr, hi = spectrum_of(sh, 0, o), spectrum_of(sh, 1, o)
            wr, wi = weight(0, i, o), weight(1, i, o)
            re = re + (wr * hr + wi * hi)
            im = im + (wr * hi - wi * hr)
        modes.append((re, im))
    synth = synth_yz(modes, eh, el)
    for c in range(C):
        at = slice(c * CELLS, (c + 1) * CELLS)
        grad_fields[at, :] = local[at, :] + dot(synth, ts[c])

    wave = lax.broadcasted_iota(jnp.int32, (MODES, 256), 0)
    factor = jnp.where(wave == 0, 1.0, 2.0).astype(f32) * (1.0 / float(N) ** 3)
    for i in range(C):
        ur, ui = spectrum_of(su, 0, i) * factor, spectrum_of(su, 1, i) * factor
        for o in range(C):
            hr, hi = spectrum_of(sh, 0, o), spectrum_of(sh, 1, o)
            pair = (ur * hr + ui * hi, ur * hi - ui * hr)
            for t in range(2):
                at = ((t * C + i) * C + o) * MODES * MODES
                for q in range(MODES):
                    grad_weights[pl.ds(at + q, MODES, stride=MODES), :] = pair[t][
                        :, q * 16 : q * 16 + 16
                    ]


def per_device(fields, cotangent, spec_weights, point_weights, bias):
    vmem = pl.BlockSpec(memory_space=pltpu.VMEM)
    smem = pl.BlockSpec(memory_space=pltpu.SMEM)
    anywhere = pl.BlockSpec(memory_space=pl.ANY)
    tile = (8, 128)
    ts = jnp.asarray(synthesis_constant())
    local, su, sh, wm, eh, el = pl.pallas_call(
        comm_kernel,
        out_shape=(
            jax.ShapeDtypeStruct((C * CELLS, N), f32),
            jax.ShapeDtypeStruct((PLANE, *tile), f32),
            jax.ShapeDtypeStruct((PLANE, *tile), f32),
            jax.ShapeDtypeStruct((512, 256), f32),
            jax.ShapeDtypeStruct((256, 512), bf16),
            jax.ShapeDtypeStruct((256, 512), bf16),
        ),
        in_specs=[anywhere] * 7 + [smem] * 2,
        out_specs=[vmem] * 6,
        scratch_shapes=[
            pltpu.VMEM((C * CELLS, N), f32),
            pltpu.VMEM((C * CELLS, N), f32),
            pltpu.VMEM((C * CELLS, N), f32),
            pltpu.VMEM((8192, 16), f32),
            pltpu.VMEM((LINES, 512), f32),
            pltpu.VMEM((LINES, 512), f32),
            pltpu.VMEM((64, N), bf16),
            pltpu.VMEM((C, 384, N), bf16),
            pltpu.VMEM((128, 256), f32),
            pltpu.VMEM((PLANE, *tile), f32),
            pltpu.VMEM((PLANE, *tile), f32),
            pltpu.VMEM((PLANE, *tile), f32),
            pltpu.VMEM((PLANE, *tile), f32),
            pltpu.VMEM((2, *tile), f32),
            pltpu.VMEM((2, *tile), f32),
            pltpu.VMEM((DEPTH, *tile), f32),
            pltpu.VMEM((DEPTH, *tile), f32),
            pltpu.VMEM((PLANE, *tile), f32),
            pltpu.VMEM((PLANE, *tile), f32),
            pltpu.SemaphoreType.DMA((10,)),
            pltpu.SemaphoreType.DMA((6,)),
            pltpu.SemaphoreType.DMA((6,)),
        ],
        compiler_params=pltpu.CompilerParams(collective_id=0, has_side_effects=True),
        name="spectra",
    )(
        fields.reshape(C * CELLS, N),
        cotangent.reshape(C * CELLS, N),
        spec_weights.reshape(8192, 16),
        jnp.asarray(signed_table(True)),
        jnp.asarray(signed_table(False)),
        jnp.asarray(analysis_constant()),
        ts,
        point_weights,
        bias,
    )
    grad_fields, grad_weights = pl.pallas_call(
        final_kernel,
        out_shape=(
            jax.ShapeDtypeStruct((C * CELLS, N), f32),
            jax.ShapeDtypeStruct((8192, 16), f32),
        ),
        in_specs=[vmem] * 7,
        out_specs=[vmem] * 2,
        name="gradients",
    )(local, su, sh, wm, eh, el, ts)
    return (
        grad_fields.reshape(1, C, LINES, LINES, N),
        grad_weights.reshape(2, C, C, MODES, MODES, MODES),
    )


def solution(mesh):
    placed = (P(None, None, "row", "col", None), P(None, None, "row", "col", None), P(), P(), P())
    return jax.shard_map(
        per_device,
        mesh=mesh,
        in_specs=placed,
        out_specs=(P(None, None, "row", "col", None), P()),
        check_vma=False,
    )
```

time: 428 us -> 51.8 us (0.12)
  waiting for transfers between devices: 291 us -> 0 us
  Pallas kernels: 0 us -> 51.1 us
  local copies, waits for them, and re-layouts: 35.6 us -> 0 us
  starting transfers between devices: 33.5 us -> 0 us
  blocking collectives: 23.2 us -> 0 us
  matrix products: 22.5 us -> 0 us
  between operations: 14.5 us -> 0.64 us
  other arithmetic: 6.94 us -> 0 us
    psum x1 -> x0, waiting for transfers between devices: 258 us -> none  [per_device(): grad_spectral = lax.psum(full_grad, ('row', 'col'))]
    pallas_call x0 -> x2, Pallas kernels: none -> 51.1 us  [the longest x1 45.5 us: per_device(): pl.pallas_call(comm_kernel, out_shape=(jax.ShapeDtypeStruct((C * CELLS, N...]
    all_to_all x6 -> x0, starting transfers between devices: 33.4 us -> none  [the longest x1 11.7 us: to_modes(): lax.all_to_all(along_x, 'row', split_axis=2, concat_axis=5, tiled=True)]
    all_to_all x6 -> x0, waiting for transfers between devices: 32.1 us -> none  [the longest x2 10.8 us: from_modes(): lax.all_to_all(along_y, 'row', split_axis=5, concat_axis=2, tiled=True)]
    all_to_all x2 -> x0, blocking collectives: 23.2 us -> none  [the longest x1 12.3 us: to_modes(): lax.all_to_all(along_x, 'row', split_axis=2, concat_axis=5, tiled=True)]
    dot_general x14 -> x0, matrix products: 22.5 us -> none  [the longest x2 8.67 us: to_modes(): jnp.einsum('bcyzx,xtp->btpczy', field, first_table(), precision=highest)]
    unnamed x26 -> x0, local copies, waits for them, and re-layouts: 18.6 us -> none
    all_to_all x8 -> x0, other arithmetic: 6.25 us -> none  [the longest x2 1.85 us: to_modes(): lax.all_to_all(along_x, 'row', split_axis=2, concat_axis=5, tiled=True)]
  transfers between devices with their start and end apart: 7 -> 0, of which waited for: 7 -> 0; matrix products, arithmetic and copies ran while one was open for 4% -> 0% of each run, Pallas kernels for 0% -> 0%
where the time goes in v1:
time: 51.8 us; the launch traced here: 51.7 us
  Pallas kernels  51.1 us (99%)
  between operations  0.64 us (1%)
    pallas_call x1, Pallas kernels, per_device(): pl.pallas_call(comm_kernel, out_shape=(jax.ShapeDtypeStruct((C * CELLS, N...  45.5 us
    pallas_call x1, Pallas kernels, per_device(): pl.pallas_call(final_kernel, out_shape=(jax.ShapeDtypeStruct((C * CELLS,...  5.54 us

profile of v1, /device:TPU:1, one launch (start us, length us, event | category | flops | bytes accessed | tf_op | source)
XLA Modules:
  0.0 51.7 jit_solution(15263401773125608940)
XLA Ops:
  0.6 45.5 %spectra.1 = (f32[1024,256]{1,0:T(8,128)}, f32[32,8,128]{2,1,0:T(8,128)}, f32[32,8,128]{2,1,0:T(8,128)}, f32[512,256]{1,0:T(8,128)}, bf16[256,512]{1,0:T(8,128)(2,1)}, /*index=5*/bf16[256,512]{1,0:T(8,128)(2,1)}) custom-call(f32[1024,256]{1,0:T(8,128)} %bitcast.6, f32[1024,256]{1,0:T(8,128)} %bitcast.7, f32[8192,16]{1,0:T(8,128)} %bitcast.5, ...), custom_call_target="tpu_custom_call" | custom-call | tf_op jit(solution)/shard_map/spectra/pallas_call | solution.py:398
  46.2 5.5 %gradients.1 = (f32[1024,256]{1,0:T(8,128)}, f32[8192,16]{1,0:T(8,128)}) custom-call(f32[1024,256]{1,0:T(8,128)} %get-tuple-element.10.local, f32[32,8,128]{2,1,0:T(8,128)} %get-tuple-element.11.su, f32[32,8,128]{2,1,0:T(8,128)} %get-tuple-element.12.sh, f32[512,256]{1,0:T(8,128)} %get-tuple-element.13.wm, bf16[256,512]{1,0:T(8,128)(2,1)} %get-tuple-element.14.eh, ...), custom_call_target="tpu_custom_call" | custom-call | tf_op jit(solution)/shard_map/gradients/pallas_call | solution.py:447
